TPU v7x, 32 devices: a whole 2x2x4 slice. The times are simulated.
32 devices in a mesh: member: 2 (over x), lat: 16 (over z, y, core).
Axes of the slice: x: 2, y: 2, z: 4, core: 2. Of those that a mesh axis runs over, the one named last changes fastest.
Arguments:
- height: float32 [128, 32, 1440], P(('member', 'lat')), parts along dimension 0, may hold values from -6 to 6
- zonal_courant: float32 [128, 32, 1440], P(('member', 'lat')), parts along dimension 0, may hold values from -1.5 to 1.5
- merid_courant: float32 [128, 32, 1440], P(('member', 'lat')), parts along dimension 0, may hold values from -1.5 to 1.5
- rates: float32 [64], P('member'), parts along dimension 0, may hold values from 0.05 to 0.5
- thresholds: float32 [64], P('member'), parts along dimension 0, may hold values from -3 to 3
- flags: int32 [64], replicated, may hold values from 0 to 1, as said below
- cutoffs: int32 [64], replicated, may hold values from 45 to 360
Outputs:
- filtered_height: float32 [128, 32, 1440], P(('member', 'lat')), parts along dimension 0
There are 2 independent parts, one for each index of `member`. A program takes and returns all parts, laid end to end along the dimension named above; an argument that names none is the same for every part. Nothing has to cross between parts.
Inputs may be any that keep to these rules, and one draw needn't show every extreme that they name: flags is 1 on a southern band of rows that starts at row 0 and on a northern band that ends at row 63, each band 64 // 8 to 16 rows long, and 0 on all other rows.
All inputs are finite; a program needn't handle non-finite values.
Results may differ from a plain program's by a relative error of at most 0.00007.
Values sent between devices are 32-bit elements; how exact they have to be, the bound alone decides.
A program may use at most 64 MiB of HBM per device.

v0:
```python
import jax
import jax.numpy as jnp
from jax import lax
from jax.sharding import PartitionSpec as P


def padded_2(cells, sides, width):
    for axis, dim in sides:
        count = lax.axis_size(axis)
        ends = count - 1
        head = lax.slice_in_dim(cells, 0, width, axis=dim)
        tail = lax.slice_in_dim(cells, cells.shape[dim] - width, cells.shape[dim], axis=dim)
        cells = jnp.concatenate(
            [
                lax.ppermute(tail, axis, [(i, (i + 1) % count) for i in range(ends)]),
                cells,
                lax.ppermute(head, axis, [((i + 1) % count, i) for i in range(ends)]),
            ],
            axis=dim,
        )
    return cells


def transform_table(nlon, nkp):
    points = jnp.arange(nlon, dtype=jnp.int32)
    waves = jnp.arange(nkp, dtype=jnp.int32)
    phase = points[:, None] * waves[None, :] % nlon
    angle = 2.0 * jnp.pi / nlon * phase.astype(jnp.float32)
    return jnp.concatenate([jnp.cos(angle), jnp.sin(angle)], axis=1)


def wave_weights(nlon, nkp):
    waves = jnp.arange(nkp, dtype=jnp.int32)
    interior = jnp.where((waves > 0) & (waves < nlon // 2), 2.0, 1.0)
    return jnp.where(waves <= nlon // 2, interior, 0.0).astype(jnp.float32) / nlon


def damping(row_flags, row_cutoffs, nkp):
    waves = jnp.maximum(jnp.arange(nkp), 1).astype(jnp.float32)
    ratio = row_cutoffs.astype(jnp.float32)[:, None] / waves[None, :]
    factor = jnp.minimum(1.0, ratio * ratio)
    return jnp.where(row_flags[:, None] > 0, factor, 1.0)


def filter_units(flat, damp, table, weights):
    highest = lax.Precision.HIGHEST
    spectrum = jnp.dot(flat, table, precision=highest, preferred_element_type=jnp.float32)
    factor = (1.0 - damp) * weights[None, :]
    scaled = spectrum * jnp.concatenate([factor, factor], axis=1)
    dims = (((1,), (1,)), ((), ()))
    removed = lax.dot_general(
        scaled, table, dims, precision=highest, preferred_element_type=jnp.float32
    )
    return flat - removed


def filtered_or_kept(block, row_flags, row_cutoffs, table, weights):
    rows, levels, nlon = block.shape
    damp = damping(row_flags, row_cutoffs, weights.shape[0])
    unit_damp = jnp.broadcast_to(damp[:, None, :], (rows, levels, damp.shape[1])).reshape(
        rows * levels, damp.shape[1]
    )

    def apply_filter(data):
        return filter_units(data.reshape(rows * levels, nlon), unit_damp, table, weights).reshape(
            rows, levels, nlon
        )

    def keep_block(data):
        return data

    return lax.cond(jnp.any(row_flags > 0), apply_filter, keep_block, block)


def face_fluxes(rows_height, rows_speed, face_cos, count):
    face_value = (
        7.0 * (rows_height[1 : count + 1] + rows_height[2 : count + 2])
        - (rows_height[0:count] + rows_height[3 : count + 3])
    ) / 12.0
    speed = 0.5 * (rows_speed[0:count] + rows_speed[1 : count + 1]) * face_cos[:, None, None]
    return speed * face_value


def face_cosines(face_ids, nlat):
    return jnp.where(
        (face_ids > 0) & (face_ids < nlat),
        jnp.sin(jnp.pi * face_ids.astype(jnp.float32) / nlat),
        jnp.float32(0.0),
    )


def local(height, zonal_courant, merid_courant, rates, thresholds, flags, cutoffs):
    lat_rows, levels, nlon = height.shape
    devices = lax.axis_size("lat")
    position = lax.axis_index("lat")
    first_row = position * lat_rows
    nlat = lat_rows * devices
    local_rows = first_row + jnp.arange(lat_rows, dtype=jnp.int32)
    cos_rows = jnp.sin(jnp.pi * (local_rows.astype(jnp.float32) + 0.5) / nlat)
    faces = first_row + jnp.arange(lat_rows + 1, dtype=jnp.int32)
    cos_faces = face_cosines(faces, nlat)
    padded = padded_2(jnp.stack([height, merid_courant]), (("lat", 1),), 2)
    east = jnp.roll(height, -1, axis=2)
    west = jnp.roll(height, 1, axis=2)
    far_east = jnp.roll(height, -2, axis=2)
    face_height = (7.0 * (height + east) - (west + far_east)) / 12.0
    face_speed = 0.5 * (zonal_courant + jnp.roll(zonal_courant, -1, axis=2))
    zonal_flux = face_speed * face_height
    zonal_div = zonal_flux - jnp.roll(zonal_flux, 1, axis=2)
    source = -rates[None, :, None] * jax.nn.softplus(height - thresholds[None, :, None])
    partial_sums = jnp.sum(jnp.sum(source, axis=2) * cos_rows[:, None], axis=0)
    totals = lax.psum(partial_sums, "lat")
    all_rows = jnp.arange(nlat, dtype=jnp.int32)
    area = nlon * jnp.sum(jnp.sin(jnp.pi * (all_rows.astype(jnp.float32) + 0.5) / nlat))
    level_mean = totals / area
    padded_height = padded[0]
    padded_speed = padded[1]
    count = lat_rows + 1
    merid_flux = face_fluxes(padded_height, padded_speed[1:], cos_faces, count)
    merid_div = (merid_flux[1:] - merid_flux[:-1]) / cos_rows[:, None, None]
    updated = height - zonal_div - merid_div + source - level_mean[None, :, None]
    nkp = (nlon // 2 + 128) // 128 * 128
    table = transform_table(nlon, nkp)
    weights = wave_weights(nlon, nkp)
    row_flags = lax.dynamic_slice_in_dim(flags, first_row, lat_rows)
    row_cutoffs = lax.dynamic_slice_in_dim(cutoffs, first_row, lat_rows)
    result = filtered_or_kept(updated, row_flags, row_cutoffs, table, weights)
    return result


def solution(mesh):
    return jax.shard_map(
        local,
        mesh=mesh,
        in_specs=(
            P(("member", "lat"), None, None),
            P(("member", "lat"), None, None),
            P(("member", "lat"), None, None),
            P("member"),
            P("member"),
            P(),
            P(),
        ),
        out_specs=P(("member", "lat"), None, None),
        check_vma=False,
    )
```

profile of v0, /device:TPU:0, one launch (start us, length us, event | category | flops | bytes accessed | tf_op | source)
XLA Modules:
  0.0 101.5 jit_solution(3019089762479028692)
XLA Ops:
  0.0 0.0 copy-start
  0.0 0.0 copy-start.2
  0.0 2.8 %fusion.17 = (f32[2,2,32,1440]{3,2,1,0:T(8,128)}, f32[2,2,32,1440]{3,2,1,0:T(8,128)}) fusion(f32[1,4,32,1440]{3,2,1,0:T(8,128)} %bitcast.21, f32[1,4,32,1440]{3,2,1,0:T(8,128)} %bitcast.27), kind=kLoop, calls=%fused_computation.33 | loop fusion | flops 368640 | bytes 2949120 | tf_op jit(solution)/shard_map/stack | solution.py:102
  2.8 3.3 %collective-permute-start = (f32[2,2,32,1440]{3,2,1,0:T(8,128)}, f32[2,2,32,1440]{3,2,1,0:T(8,128)}, u32[]{:S(2)}, u32[]{:S(2)}) collective-permute-start(f32[2,2,32,1440]{3,2,1,0:T(8,128)} %get-tuple-element.115), channel_id=1, source_target_pairs={{0,1},{1,2},{2,3},{3,4},{4,5},{5,6},{6,7},{7,8},{8,9},{9,10},{10,1... | collective-permute-start | bytes 2211848 | tf_op jit(solution)/shard_map/ppermute | solution.py:15
  6.1 1.3 %collective-permute-start.1 = (f32[2,2,32,1440]{3,2,1,0:T(8,128)}, f32[2,2,32,1440]{3,2,1,0:T(8,128)}, u32[]{:S(2)}, u32[]{:S(2)}) collective-permute-start(f32[2,2,32,1440]{3,2,1,0:T(8,128)} %get-tuple-element.116), channel_id=1, source_target_pairs={{1,0},{2,1},{3,2},{4,3},{5,4},{6,5},{7,6},{8,7},{9,8},{10,9},{11,1... | collective-permute-start | bytes 2211848 | tf_op jit(solution)/shard_map/ppermute | solution.py:17
  7.3 2.8 %fusion.33 = (f32[4,32,1439]{2,1,0:T(8,128)}, f32[4,32,1439]{2,1,0:T(8,128)}) fusion(f32[4,32,1440]{2,1,0:T(8,128)} %param.9), kind=kLoop, calls=%fused_computation.63 | loop fusion | bytes 2947072 | tf_op jit(solution)/shard_map/jit(_roll_static)/slice | solution.py:104
  10.1 0.0 copy-done
  10.1 0.1 fusion.32
  10.2 0.3 slice.95
  10.5 0.0 copy-done.2
  10.5 1.2 %slice.89 = f32[4,32,1439]{2,1,0:T(8,128)} slice(f32[4,32,1440]{2,1,0:T(8,128)S(1)} %copy-done.2), slice={[0:4], [0:32], [1:1440]} | slice | bytes 1473536 | tf_op jit(solution)/shard_map/jit(_roll_static)/slice | solution.py:107
  11.8 0.7 sine_reduce_fusion
  12.4 0.0 slice-start
  12.4 0.0 copy-start.3
  12.4 0.0 copy-start.4
  12.4 0.0 copy-start.5
  12.4 0.0 copy-start.7
  12.5 19.6 %fusion.7 = (f32[1440,768]{1,0:T(8,128)}, f32[1440,768]{1,0:T(8,128)}) fusion(), kind=kLoop, calls=%fused_computation.15 | loop fusion | flops 9953280 | bytes 8847360 | tf_op jit(solution)/shard_map/sin | solution.py:29
  32.0 0.0 copy-done.9
  32.1 0.0 slice-done
  32.1 0.0 copy-done.3
  32.1 0.0 copy-done.4
  32.1 0.0 copy-done.5
  32.1 0.0 copy-done.7
  32.1 0.9 fusion.29
  33.0 0.1 multiply_reduce_fusion
  33.1 35.8 %psum.7 = f32[32]{0:T(128)S(1)} all-reduce(f32[32]{0:T(128)S(1)} %multiply_reduce_fusion), channel_id=1, replica_groups=mesh['member'=2,'lat'=16] {'lat'}, use_global_device_ids=true, to_apply=%region_3.4 | all-reduce | flops 32 | bytes 256 | tf_op jit(solution)/shard_map/psum | solution.py:112
  68.9 0.1 slice.109
  69.0 0.0 copy-done.8
  69.0 0.8 fusion.31
  69.8 0.0 copy-done.10
  69.8 0.1 dynamic-slice_convert_fusion
  71.2 0.0 copy-start.6
  71.2 8.2 %pad_maximum_fusion = f32[1440,1536]{1,0:T(8,128)} fusion(f32[1440,768]{1,0:T(8,128)} %get-tuple-element.123, f32[1440,768]{1,0:T(8,128)} %get-tuple-element.124), kind=kLoop, calls=%fused_computation.8 | loop fusion | flops 2211840 | bytes 17694720 | tf_op jit(solution)/shard_map/concatenate | solution.py:29
  79.4 0.0 collective-permute-done
  79.4 0.0 collective-permute-done.1
  79.4 0.0 copy-done.6
  79.4 1.9 %maximum_maximum_fusion = (f32[2,6,32,1440]{3,2,1,0:T(8,128)S(1)}, f32[2,6,32,1440]{3,2,1,0:T(8,128)S(1)}) fusion(f32[1,4,32,1440]{3,2,1,0:T(8,128)S(1)} %bitcast.28, f32[1,4,32,1440]{3,2,1,0:T(8,128)S(1)} %bitcast.22, f32[2,2,32,1440]{3,2,1,0:T(8,128)} %collective-permute-done, f32[2,2,32,1440]{3,2,1,0:T(8,128)} %collective-permute-done.1), kind=kLoop, calls=%fused_computation.18 | loop fusion | flops 2211840 | bytes 7372800 | tf_op jit(solution)/shard_map/concatenate | solution.py:13
  81.3 0.5 fusion.13
  81.8 0.7 fusion.22
  82.6 18.0 %conditional.1 = (f32[4,32,1440]{2,1,0:T(8,128)S(1)}) conditional(s32[]{:T(128)} %convert_element_type.42, f32[4,32,1440]{2,1,0:T(8,128)S(1)} %fusion.22, (f32[4,32,1440]{2,1,0:T(8,128)S(1)}, f32[1440,1536]{1,0:T(8,128)}, pred[4]{0:T(512)(128)(4,1)S(1)}, f32[4]{0:T(128)S(1)}, f32[1,768]{1,0:T(1,128)S(1)}, /*index=5*/s32[768]{0:T(1024)S(1)}) %tuple.45), branch_computations={%region_5.6_spmd, %region_6.7_spmd} | conditional | flops 6795468800 | bytes 25258016 | solution.py:72
  82.8 0.1 fusion.2
  82.9 7.6 %convolution_multiply_fusion = f32[128,1536]{1,0:T(8,128)S(1)} fusion(f32[128,1440]{1,0:T(8,128)S(1)} %bitcast.24, f32[1440,1536]{1,0:T(8,128)} %get-tuple-element.105, f32[128,768]{1,0:T(8,128)S(1)} %bitcast_multiply_fusion), kind=kOutput, calls=%fused_computation.1 | convolution fusion | flops 3397779456 | bytes 10764288 | tf_op jit(solution)/shard_map/cond/branch_1_fun/dot_general | solution.py:47
  90.6 0.3 copy.27
  90.8 9.5 %convolution_subtract_fusion = f32[128,1440]{0,1:T(8,128)S(1)} fusion(f32[128,1440]{0,1:T(8,128)S(1)} %copy.27, f32[128,1536]{1,0:T(8,128)S(1)} %convolution_multiply_fusion, f32[1440,1536]{1,0:T(8,128)} %get-tuple-element.105), kind=kOutput, calls=%fused_computation | convolution fusion | flops 3397570560 | bytes 11108352 | tf_op jit(solution)/shard_map/cond/branch_1_fun/dot_general | solution.py:51
  100.3 0.3 copy.28
  100.6 0.0 copy-start.1
  100.6 0.9 copy-done.1
  (13 shorter events, 0.2 us)
Async XLA Ops:
  0.0 10.1 %copy-start = (f32[4,32,1440]{2,1,0:T(8,128)S(1)}, f32[4,32,1440]{2,1,0:T(8,128)}, u32[]{:S(2)}) copy-start(f32[4,32,1440]{2,1,0:T(8,128)} %param.9) | copy-start | bytes 2211844
  0.0 10.5 %copy-start.2 = (f32[4,32,1440]{2,1,0:T(8,128)S(1)}, f32[4,32,1440]{2,1,0:T(8,128)}, u32[]{:S(2)}) copy-start(f32[4,32,1440]{2,1,0:T(8,128)} %param.10) | copy-start | bytes 2211844
  2.8 76.6 %collective-permute-start = (f32[2,2,32,1440]{3,2,1,0:T(8,128)}, f32[2,2,32,1440]{3,2,1,0:T(8,128)}, u32[]{:S(2)}, u32[]{:S(2)}) collective-permute-start(f32[2,2,32,1440]{3,2,1,0:T(8,128)} %get-tuple-element.115), channel_id=1, source_target_pairs={{0,1},{1,2},{2,3},{3,4},{4,5},{5,6},{6,7},{7,8},{8,9},{9,10},{10,1... | collective-permute-start | bytes 2211848 | tf_op jit(solution)/shard_map/ppermute | solution.py:15
  6.1 73.3 %collective-permute-start.1 = (f32[2,2,32,1440]{3,2,1,0:T(8,128)}, f32[2,2,32,1440]{3,2,1,0:T(8,128)}, u32[]{:S(2)}, u32[]{:S(2)}) collective-permute-start(f32[2,2,32,1440]{3,2,1,0:T(8,128)} %get-tuple-element.116), channel_id=1, source_target_pairs={{1,0},{2,1},{3,2},{4,3},{5,4},{6,5},{7,6},{8,7},{9,8},{10,9},{11,1... | collective-permute-start | bytes 2211848 | tf_op jit(solution)/shard_map/ppermute | solution.py:17
  12.4 19.6 %copy-start.9 = (f32[32]{0:T(128)S(1)}, f32[32]{0:T(128)}, u32[]{:S(2)}) copy-start(f32[32]{0:T(128)} %param.12) | copy-start | bytes 388
  12.4 19.6 %slice-start = ((f32[4,32,1440]{2,1,0:T(8,128)}), f32[4,32,1]{2,1,0:T(8,128)S(1)}, s32[]{:S(2)}) async-start(f32[4,32,1440]{2,1,0:T(8,128)} %param.10), calls=%async_computation | async-start | bytes 131072 | tf_op jit(solution)/shard_map/jit(_roll_static)/slice | solution.py:107
  12.4 19.7 %copy-start.3 = (f32[4,32,1439]{2,1,0:T(8,128)S(1)}, f32[4,32,1439]{2,1,0:T(8,128)}, u32[]{:S(2)}) copy-start(f32[4,32,1439]{2,1,0:T(8,128)} %slice.89) | copy-start | bytes 2210308
  12.4 19.7 %copy-start.4 = (f32[4,32,1439]{2,1,0:T(8,128)S(1)}, f32[4,32,1439]{2,1,0:T(8,128)}, u32[]{:S(2)}) copy-start(f32[4,32,1439]{2,1,0:T(8,128)} %get-tuple-element.121) | copy-start | bytes 2210308
  12.4 19.7 %copy-start.5 = (f32[4,32,1439]{2,1,0:T(8,128)S(1)}, f32[4,32,1439]{2,1,0:T(8,128)}, u32[]{:S(2)}) copy-start(f32[4,32,1439]{2,1,0:T(8,128)} %get-tuple-element.122) | copy-start | bytes 2210308
  12.4 19.7 %copy-start.7 = (f32[32]{0:T(128)S(1)}, f32[32]{0:T(128)}, u32[]{:S(2)}) copy-start(f32[32]{0:T(128)} %param.13) | copy-start | bytes 388
  32.0 37.0 %copy-start.8 = (s32[64]{0:T(128)S(1)}, s32[64]{0:T(128)}, u32[]{:S(2)}) copy-start(s32[64]{0:T(128)} %param.14) | copy-start | bytes 772
  32.0 37.8 %copy-start.10 = (s32[64]{0:T(128)S(1)}, s32[64]{0:T(128)}, u32[]{:S(2)}) copy-start(s32[64]{0:T(128)} %param.15) | copy-start | bytes 772
  71.2 8.2 %copy-start.6 = (f32[4,32,1440]{2,1,0:T(8,128)S(1)}, f32[4,32,1440]{2,1,0:T(8,128)}, u32[]{:S(2)}) copy-start(f32[4,32,1440]{2,1,0:T(8,128)} %param.11) | copy-start | bytes 2211844
  100.6 0.9 copy-start.1
where the time goes:
time: 102 us; the launch traced here: 101 us
  other arithmetic  36.4 us (36%)
  blocking collectives  35.8 us (35%)
  matrix products  17.1 us (17%)
  local copies, waits for them, and re-layouts  5.82 us (6%)
  starting transfers between devices  4.55 us (4%)
  between operations  1.52 us (1%)
    psum x1, blocking collectives, local(): totals = lax.psum(partial_sums, 'lat')  35.8 us
    sin x1, other arithmetic, transform_table(): return jnp.concatenate([jnp.cos(angle), jnp.sin(angle)], axis=1)  19.6 us
    dot_general x1, matrix products, filter_units(): lax.dot_general(scaled, table, dims, precision=highest, preferred_element...  9.48 us
    concatenate x1, other arithmetic, transform_table(): return jnp.concatenate([jnp.cos(angle), jnp.sin(angle)], axis=1)  8.16 us
    dot_general x1, matrix products, filter_units(): jnp.dot(flat, table, precision=highest, preferred_element_type=jnp.float32)  7.64 us
    ppermute x1, starting transfers between devices, padded_2(): lax.ppermute(tail, axis, [(i, (i + 1) % count) for i in range(ends)])  3.27 us
    slice x2, local copies, waits for them, and re-layouts, local(): west = jnp.roll(height, 1, axis=2)  2.85 us
    another operation x1, other arithmetic, local(): padded = padded_2(jnp.stack([height, merid_courant]), (('lat', 1),), 2)  2.78 us
  transfers between devices with their start and end apart: 2, of which 0 were waited for; matrix products, arithmetic and copies ran while one was open for 34% of the time, Pallas kernels for 0%

commit v1 on v0

v1 whole, which is shorter than its diff:
```python
import functools

import jax
import jax.numpy as jnp
import numpy as np
from jax import lax
from jax.experimental import pallas as pl
from jax.experimental.pallas import tpu as pltpu
from jax.sharding import PartitionSpec as P

CHUNKS = 2
GROUP = 8
BF = jnp.bfloat16
F32 = jnp.float32


def split_table(table):
    high = table.astype(jnp.bfloat16)
    low = (table - high.astype(np.float64)).astype(jnp.bfloat16)
    return np.stack([high, low])


def cas(angle):
    return np.cos(angle) + np.sin(angle)


def filter_tables(nlon):
    quarter, half = nlon // 4, nlon // 2
    m = np.arange(quarter)
    zero = cas(2 * np.pi * (np.outer(m, m) % quarter) / quarter)
    odd = 2 * np.arange(half) + 1
    two = cas(2 * np.pi * (np.outer(odd[:quarter], odd[:quarter]) % nlon) / nlon)
    ones = cas(np.pi * (np.outer(odd, odd) % (2 * nlon)) / nlon)
    return split_table(np.stack([zero, two], 0)), split_table(ones)


def latitude_table(nlat):
    rows = np.sin(np.pi * (np.arange(nlat) + 0.5) / nlat)
    faces = np.sin(np.pi * np.arange(nlat + 1) / nlat)
    faces[0] = faces[-1] = 0.0
    table = np.zeros((3, nlat + 1), np.float32)
    table[0] = faces / 24.0
    table[1, :nlat] = rows
    table[2, :nlat] = 1.0 / rows
    return table, float(np.sum(rows))


def shifted(x, s):
    return jnp.concatenate([x[:, s:], x[:, :s]], axis=1)


def halves(x):
    high = x.astype(BF)
    return high, (x - high.astype(F32)).astype(BF)


def product(x, high_table, low_table):
    high, low = halves(x)
    rows = x.shape[0]
    both = jnp.dot(
        jnp.concatenate([high, low], axis=0), high_table, preferred_element_type=F32
    )
    return both[:rows] + both[rows:] + jnp.dot(high, low_table, preferred_element_type=F32)


def kernel(
    n, area,
    lat_ref, flags_ref, cutoffs_ref, rates_ref, thresholds_ref,
    h_hbm, z_hbm, m_hbm, quarter_hbm, half_hbm,
    out_hbm,
    h, z, m, quarter_t, half_t, base, result, sides, part, mine, others,
    hl, ml, hr, mr,
    in_sem, out_sem, halo_send, halo_recv, sum_send, sum_recv,
):
    rows, levels, nlon = h.shape
    me = lax.axis_index("lat")
    first = me * rows
    groups = levels // GROUP
    width = levels // CHUNKS

    loads = [
        pltpu.make_async_copy(src, dst, in_sem.at[i])
        for i, (src, dst) in enumerate(
            [(h_hbm, h), (z_hbm, z), (m_hbm, m), (quarter_hbm, quarter_t), (half_hbm, half_t)]
        )
    ]
    for load in loads:
        load.start()

    barrier = pltpu.get_barrier_semaphore()

    def greet(o, c):
        pl.semaphore_signal(barrier, inc=1, device_id={"lat": lax.rem(me + o, n)})
        return c

    lax.fori_loop(1, n, greet, 0)
    pl.semaphore_wait(barrier, n - 1)

    def halo_copies(c, side):
        at = pl.ds(c * width, width)
        if side == 0:
            pairs = [
                (h_hbm.at[pl.ds(rows - 2, 2), at], hl.at[:, at]),
                (m_hbm.at[rows - 1, at], ml.at[at]),
            ]
            target = me + 1
        else:
            pairs = [
                (h_hbm.at[pl.ds(0, 2), at], hr.at[:, at]),
                (m_hbm.at[0, at], mr.at[at]),
            ]
            target = me - 1
        return [
            pltpu.make_async_remote_copy(
                src, dst, halo_send.at[side, c, i], halo_recv.at[side, c, i],
                device_id={"lat": target},
            )
            for i, (src, dst) in enumerate(pairs)
        ]

    def start_halo(side):
        for c in range(CHUNKS):
            for copy in halo_copies(c, side):
                copy.start()

    pl.when(me < n - 1)(lambda: start_halo(0))
    pl.when(me > 0)(lambda: start_halo(1))

    @pl.when(me == 0)
    def _():
        hl[...] = jnp.zeros_like(hl)
        ml[...] = jnp.zeros_like(ml)

    @pl.when(me == n - 1)
    def _():
        hr[...] = jnp.zeros_like(hr)
        mr[...] = jnp.zeros_like(mr)

    lane = lax.broadcasted_iota(jnp.int32, (levels, levels), 1)
    diagonal = lane == lax.broadcasted_iota(jnp.int32, (levels, levels), 0)

    def column(row):
        spread = jnp.where(diagonal, jnp.broadcast_to(row, (levels, levels)), 0.0)
        return jnp.sum(spread, axis=1, keepdims=True)

    sides[0] = jnp.broadcast_to(column(rates_ref[...]), (levels, 128))
    sides[1] = jnp.broadcast_to(column(thresholds_ref[...]), (levels, 128))

    loads[0].wait()
    loads[1].wait()

    def local_terms(g, carry):
        at = pl.ds(pl.multiple_of(g * GROUP, GROUP), GROUP)
        rate = sides[0, at, :][:, :1]
        threshold = sides[1, at, :][:, :1]
        weighted = jnp.zeros((GROUP, nlon), F32)
        for r in range(rows):
            hh = h[r, at, :]
            zz = z[r, at, :]
            face = 7.0 * (hh + shifted(hh, 1)) - (shifted(hh, nlon - 1) + shifted(hh, 2))
            flux = (zz + shifted(zz, 1)) * face * (1.0 / 24.0)
            source = -rate * jnp.log(1.0 + jnp.exp(hh - threshold))
            base[r, at, :] = hh - (flux - shifted(flux, nlon - 1)) + source
            weighted = weighted + source * lat_ref[1, first + r]
        total = jnp.sum(weighted, axis=1, keepdims=True)
        part[at, :] = jnp.broadcast_to(total, (GROUP, 128))
        return carry

    lax.fori_loop(0, groups, local_terms, 0)

    wide = lax.broadcasted_iota(jnp.int32, (levels, 128), 1)
    tall = lax.broadcasted_iota(jnp.int32, (levels, 128), 0)
    mine[...] = jnp.sum(jnp.where(wide == tall, part[...], 0.0), axis=0, keepdims=True)

    def sum_copy(o):
        return pltpu.make_async_remote_copy(
            mine, others.at[o - 1], sum_send.at[o - 1], sum_recv.at[o - 1],
            device_id={"lat": lax.rem(me + o, n)},
        )

    def send_sum(o, c):
        sum_copy(o).start()
        return c

    lax.fori_loop(1, n, send_sum, 0)

    quarter, half = nlon // 4, nlon // 2

    def factors(length, step, offset):
        k = lax.broadcasted_iota(jnp.int32, (1, length), 1) * step + offset
        k = jnp.maximum(jnp.minimum(k, nlon - k), 1).astype(F32)
        out = []
        for r in range(rows):
            ratio = cutoffs_ref[first + r].astype(F32) / k
            factor = (1.0 - jnp.minimum(1.0, ratio * ratio)) * (1.0 / nlon)
            on = jnp.where(flags_ref[first + r] > 0, 1.0, 0.0)
            out.append(factor * on)
        return out

    all_factors = [factors(quarter, 4, 0), factors(quarter, 4, 2), factors(half, 2, 1)]

    def removed(x, high_table, low_table, factor):
        spectrum = product(x, high_table, low_table).reshape(rows, width, x.shape[1])
        scaled = jnp.concatenate([spectrum[r] * factor[r] for r in range(rows)], axis=0)
        return product(scaled, high_table, low_table)

    loads[2].wait()

    def merid(c):
        def body(g, carry):
            at = pl.ds(pl.multiple_of(c * width + g * GROUP, GROUP), GROUP)

            def height(i):
                return hl[i + 2, at, :] if i < 0 else hr[i - rows, at, :] if i >= rows else h[i, at, :]

            def speed(i):
                return ml[at, :] if i < 0 else mr[at, :] if i >= rows else m[i, at, :]

            previous = None
            for f in range(rows + 1):
                face = 7.0 * (height(f - 1) + height(f)) - (height(f - 2) + height(f + 1))
                flux = (speed(f - 1) + speed(f)) * face * lat_ref[0, first + f]
                if f > 0:
                    base[f - 1, at, :] -= (flux - previous) * lat_ref[2, first + f - 1]
                previous = flux
            return carry

        lax.fori_loop(0, width // GROUP, body, 0)

    mean = None
    stores = []
    for c in range(CHUNKS):
        @pl.when(me > 0)
        def _():
            for copy in halo_copies(c, 0):
                copy.wait_recv()

        @pl.when(me < n - 1)
        def _():
            for copy in halo_copies(c, 1):
                copy.wait_recv()

        merid(c)
        if c == 0:
            loads[3].wait()
            loads[4].wait()
        at = pl.ds(c * width, width)
        x = base[:, at, :].reshape(rows * width, nlon)
        near, far = x[:, :half], x[:, half:]
        even, odd = near + far, near - far
        left, right = even[:, :quarter], even[:, quarter:]
        zero = removed(left + right, quarter_t[0, 0], quarter_t[1, 0], all_factors[0])
        two = removed(left - right, quarter_t[0, 1], quarter_t[1, 1], all_factors[1])
        ones = removed(odd, half_t[0], half_t[1], all_factors[2])
        even = jnp.concatenate([zero + two, zero - two], axis=1)
        if c == 0:
            def wait_sum(o, carry):
                sum_copy(o).wait()
                return carry

            lax.fori_loop(1, n, wait_sum, 0)
            total = mine[...] + jnp.sum(others[...], axis=0)
            mean = column(total[:, :levels]) * (1.0 / area)
        kept = jnp.concatenate([near - even - ones, far - even + ones], axis=1)
        kept = kept.reshape(rows, width, nlon) - mean[c * width : (c + 1) * width][None]
        result[:, at, :] = kept
        store = pltpu.make_async_copy(result.at[:, at], out_hbm.at[:, at], out_sem.at[c])
        store.start()
        stores.append(store)

    def finish_halo(side):
        for c in range(CHUNKS):
            for copy in halo_copies(c, side):
                copy.wait_send()

    pl.when(me < n - 1)(lambda: finish_halo(0))
    pl.when(me > 0)(lambda: finish_halo(1))
    for store in stores:
        store.wait()


def local(n, height, zonal_courant, merid_courant, rates, thresholds, flags, cutoffs):
    rows, levels, nlon = height.shape
    table, row_sum = latitude_table(rows * n)
    quarter_t, half_t = filter_tables(nlon)
    smem = pl.BlockSpec(memory_space=pltpu.SMEM)
    vmem = pl.BlockSpec(memory_space=pltpu.VMEM)
    hbm = pl.BlockSpec(memory_space=pl.ANY)
    block = pltpu.VMEM(height.shape, F32)
    return pl.pallas_call(
        functools.partial(kernel, n, nlon * row_sum),
        out_shape=jax.ShapeDtypeStruct(height.shape, F32),
        in_specs=[smem] * 3 + [vmem] * 2 + [hbm] * 5,
        out_specs=hbm,
        scratch_shapes=[
            block, block, block,
            pltpu.VMEM(quarter_t.shape, BF),
            pltpu.VMEM(half_t.shape, BF),
            block, block,
            pltpu.VMEM((2, levels, 128), F32),
            pltpu.VMEM((levels, 128), F32),
            pltpu.VMEM((1, 128), F32),
            pltpu.VMEM((n - 1, 1, 128), F32),
            pltpu.VMEM((2, levels, nlon), F32),
            pltpu.VMEM((levels, nlon), F32),
            pltpu.VMEM((2, levels, nlon), F32),
            pltpu.VMEM((levels, nlon), F32),
            pltpu.SemaphoreType.DMA((5,)),
            pltpu.SemaphoreType.DMA((CHUNKS,)),
            pltpu.SemaphoreType.DMA((2, CHUNKS, 2)),
            pltpu.SemaphoreType.DMA((2, CHUNKS, 2)),
            pltpu.SemaphoreType.DMA((n - 1,)),
            pltpu.SemaphoreType.DMA((n - 1,)),
        ],
        compiler_params=pltpu.CompilerParams(
            collective_id=0, has_side_effects=True, vmem_limit_bytes=48 * 1024 * 1024
        ),
    )(
        jnp.asarray(table), flags, cutoffs, rates[None, :], thresholds[None, :],
        height, zonal_courant, merid_courant, jnp.asarray(quarter_t), jnp.asarray(half_t),
    )


def solution(mesh):
    return jax.shard_map(
        functools.partial(local, mesh.shape["lat"]),
        mesh=mesh,
        in_specs=(
            P(("member", "lat"), None, None),
            P(("member", "lat"), None, None),
            P(("member", "lat"), None, None),
            P("member"),
            P("member"),
            P(),
            P(),
        ),
        out_specs=P(("member", "lat"), None, None),
        check_vma=False,
    )
```

time: 102 us -> 32.1 us (0.31)
  the two profiles are of different devices: /device:TPU:0 before, /device:TPU:5 now
where the time goes in v1:
time: 32.1 us; the launch traced here: 31.8 us
  Pallas kernels  23 us (72%)
  local copies, waits for them, and re-layouts  8.82 us (27%)
    pallas_call x1, Pallas kernels, local(): pl.pallas_call(functools.partial(kernel, n, nlon * row_sum), out_shape=ja...  23 us
    unnamed x19, local copies, waits for them, and re-layouts  8.82 us

profile of v1, /device:TPU:5, one launch (start us, length us, event | category | flops | bytes accessed | tf_op | source)
XLA Modules:
  0.0 31.8 jit_solution(12054552071534112133)
XLA Ops:
  0.0 0.0 copy-start
  0.0 1.2 %copy-done = bf16[2,2,360,360]{3,2,1,0:T(8,128)(2,1)S(1)} copy-done((bf16[2,2,360,360]{3,2,1,0:T(8,128)(2,1)S(1)}, bf16[2,2,360,360]{3,2,1,0:T(8,128)(2,1)}, u32[]{:S(2)}) %copy-start) | copy-done | bytes 1036824
  1.2 0.0 copy-start.1
  1.2 1.1 %copy-done.1 = f32[4,32,1440]{2,1,0:T(8,128)S(1)} copy-done((f32[4,32,1440]{2,1,0:T(8,128)S(1)}, f32[4,32,1440]{2,1,0:T(8,128)}, u32[]{:S(2)}) %copy-start.1) | copy-done | bytes 737304
  2.4 0.0 copy-start.2
  2.4 1.1 %copy-done.2 = f32[4,32,1440]{2,1,0:T(8,128)S(1)} copy-done((f32[4,32,1440]{2,1,0:T(8,128)S(1)}, f32[4,32,1440]{2,1,0:T(8,128)}, u32[]{:S(2)}) %copy-start.2) | copy-done | bytes 737304
  3.5 0.0 copy-start.3
  3.5 1.1 %copy-done.3 = f32[4,32,1440]{2,1,0:T(8,128)S(1)} copy-done((f32[4,32,1440]{2,1,0:T(8,128)S(1)}, f32[4,32,1440]{2,1,0:T(8,128)}, u32[]{:S(2)}) %copy-start.3) | copy-done | bytes 737304
  4.6 0.0 copy-start.4
  4.6 0.7 %copy-done.4 = f32[3,65]{1,0:T(4,128)S(1)} copy-done((f32[3,65]{1,0:T(4,128)S(1)}, f32[3,65]{1,0:T(4,128)}, u32[]{:S(2)}) %copy-start.4) | copy-done | bytes 804
  5.3 0.0 copy-start.5
  5.3 0.7 %copy-done.5 = s32[64]{0:T(128)S(1)} copy-done((s32[64]{0:T(128)S(1)}, s32[64]{0:T(128)}, u32[]{:S(2)}) %copy-start.5) | copy-done | bytes 280
  6.0 0.0 copy-start.6
  6.0 0.7 %copy-done.6 = s32[64]{0:T(128)S(1)} copy-done((s32[64]{0:T(128)S(1)}, s32[64]{0:T(128)}, u32[]{:S(2)}) %copy-start.6) | copy-done | bytes 280
  6.6 0.0 copy-start.7
  6.6 0.7 %copy-done.7 = f32[32]{0:T(128)S(1)} copy-done((f32[32]{0:T(128)S(1)}, f32[32]{0:T(128)}, u32[]{:S(2)}) %copy-start.7) | copy-done | bytes 152
  7.3 0.0 copy-start.8
  7.3 0.7 %copy-done.8 = f32[32]{0:T(128)S(1)} copy-done((f32[32]{0:T(128)S(1)}, f32[32]{0:T(128)}, u32[]{:S(2)}) %copy-start.8) | copy-done | bytes 152
  8.0 23.0 %shard_map.100 = f32[4,32,1440]{2,1,0:T(8,128)S(1)} custom-call(f32[3,65]{1,0:T(4,128)S(1)} %copy-done.4, s32[64]{0:T(128)S(1)} %copy-done.5, s32[64]{0:T(128)S(1)} %copy-done.6, f32[1,32]{1,0:T(1,128)S(1)} %bitcast.2, f32[1,32]{1,0:T(1,128)S(1)} %bitcast.3, f32[4,32,1440]{2,1,0:T(8,128)S(1)} %copy-done.1, f32[4,32,1440]{2,1,0:T(8,128)S(1)} %copy-done.2, ...), custom_call_target="tpu_custom_call" | custom-call | tf_op jit(solution)/shard_map/pallas_call | solution.py:290
  30.9 0.9 %copy.12 = f32[4,32,1440]{2,1,0:T(8,128)} copy(f32[4,32,1440]{2,1,0:T(8,128)S(1)} %shard_map.100) | data formatting | bytes 1474560
Async XLA Ops:
  0.0 1.2 %copy-start = (bf16[2,2,360,360]{3,2,1,0:T(8,128)(2,1)S(1)}, bf16[2,2,360,360]{3,2,1,0:T(8,128)(2,1)}, u32[]{:S(2)}) copy-start(bf16[2,2,360,360]{3,2,1,0:T(8,128)(2,1)} %constant.7.clone.quarter_hbm) | copy-start | bytes 3110404
  1.2 1.1 %copy-start.1 = (f32[4,32,1440]{2,1,0:T(8,128)S(1)}, f32[4,32,1440]{2,1,0:T(8,128)}, u32[]{:S(2)}) copy-start(f32[4,32,1440]{2,1,0:T(8,128)} %h_hbm.1) | copy-start | bytes 2211844
  2.4 1.1 %copy-start.2 = (f32[4,32,1440]{2,1,0:T(8,128)S(1)}, f32[4,32,1440]{2,1,0:T(8,128)}, u32[]{:S(2)}) copy-start(f32[4,32,1440]{2,1,0:T(8,128)} %z_hbm.1) | copy-start | bytes 2211844
  3.5 1.1 %copy-start.3 = (f32[4,32,1440]{2,1,0:T(8,128)S(1)}, f32[4,32,1440]{2,1,0:T(8,128)}, u32[]{:S(2)}) copy-start(f32[4,32,1440]{2,1,0:T(8,128)} %m_hbm.1) | copy-start | bytes 2211844
  4.6 0.7 %copy-start.4 = (f32[3,65]{1,0:T(4,128)S(1)}, f32[3,65]{1,0:T(4,128)}, u32[]{:S(2)}) copy-start(f32[3,65]{1,0:T(4,128)} %constant.6.clone.lat_ref) | copy-start | bytes 2344
  5.3 0.7 %copy-start.5 = (s32[64]{0:T(128)S(1)}, s32[64]{0:T(128)}, u32[]{:S(2)}) copy-start(s32[64]{0:T(128)} %flags_ref.1) | copy-start | bytes 772
  6.0 0.7 %copy-start.6 = (s32[64]{0:T(128)S(1)}, s32[64]{0:T(128)}, u32[]{:S(2)}) copy-start(s32[64]{0:T(128)} %cutoffs_ref.1) | copy-start | bytes 772
  6.6 0.7 %copy-start.7 = (f32[32]{0:T(128)S(1)}, f32[32]{0:T(128)}, u32[]{:S(2)}) copy-start(f32[32]{0:T(128)} %param.13) | copy-start | bytes 388
  7.3 0.7 %copy-start.8 = (f32[32]{0:T(128)S(1)}, f32[32]{0:T(128)}, u32[]{:S(2)}) copy-start(f32[32]{0:T(128)} %param.14) | copy-start | bytes 388

commit v2 on v1

--- a/solution.py
+++ b/solution.py
@@ -38,10 +38,7 @@
     rows = np.sin(np.pi * (np.arange(nlat) + 0.5) / nlat)
     faces = np.sin(np.pi * np.arange(nlat + 1) / nlat)
     faces[0] = faces[-1] = 0.0
-    table = np.zeros((3, nlat + 1), np.float32)
-    table[0] = faces / 24.0
-    table[1, :nlat] = rows
-    table[2, :nlat] = 1.0 / rows
+    table = np.concatenate([faces / 24.0, rows, 1.0 / rows]).astype(np.float32)
     return table, float(np.sum(rows))
 
 
@@ -65,9 +62,10 @@
 
 def kernel(
     n, area,
-    lat_ref, flags_ref, cutoffs_ref, rates_ref, thresholds_ref,
+    lat_hbm, flags_hbm, cutoffs_hbm, rates_hbm, thresholds_hbm,
     h_hbm, z_hbm, m_hbm, quarter_hbm, half_hbm,
     out_hbm,
+    lat_ref, flags_ref, cutoffs_ref, rates_ref, thresholds_ref,
     h, z, m, quarter_t, half_t, base, result, sides, part, mine, others,
     hl, ml, hr, mr,
     in_sem, out_sem, halo_send, halo_recv, sum_send, sum_recv,
@@ -81,11 +79,25 @@
     loads = [
         pltpu.make_async_copy(src, dst, in_sem.at[i])
         for i, (src, dst) in enumerate(
-            [(h_hbm, h), (z_hbm, z), (m_hbm, m), (quarter_hbm, quarter_t), (half_hbm, half_t)]
+            [
+                (h_hbm, h), (z_hbm, z), (m_hbm, m), (quarter_hbm, quarter_t), (half_hbm, half_t),
+                (lat_hbm, lat_ref), (flags_hbm, flags_ref), (cutoffs_hbm, cutoffs_ref),
+                (rates_hbm, rates_ref), (thresholds_hbm, thresholds_ref),
+            ]
         )
     ]
-    for load in loads:
-        load.start()
+    for i in (0, 2, 1, 5, 6, 7, 8, 9):
+        loads[i].start()
+    nlat = rows * n
+
+    def face_scale(f):
+        return lat_ref[first + f]
+
+    def row_weight(r):
+        return lat_ref[nlat + 1 + first + r]
+
+    def row_scale(r):
+        return lat_ref[2 * nlat + 1 + first + r]
 
     barrier = pltpu.get_barrier_semaphore()
 
@@ -100,14 +112,14 @@
         at = pl.ds(c * width, width)
         if side == 0:
             pairs = [
-                (h_hbm.at[pl.ds(rows - 2, 2), at], hl.at[:, at]),
-                (m_hbm.at[rows - 1, at], ml.at[at]),
+                (h.at[pl.ds(rows - 2, 2), at], hl.at[:, at]),
+                (m.at[rows - 1, at], ml.at[at]),
             ]
             target = me + 1
         else:
             pairs = [
-                (h_hbm.at[pl.ds(0, 2), at], hr.at[:, at]),
-                (m_hbm.at[0, at], mr.at[at]),
+                (h.at[pl.ds(0, 2), at], hr.at[:, at]),
+                (m.at[0, at], mr.at[at]),
             ]
             target = me - 1
         return [
@@ -123,8 +135,12 @@
             for copy in halo_copies(c, side):
                 copy.start()
 
+    loads[0].wait()
+    loads[2].wait()
     pl.when(me < n - 1)(lambda: start_halo(0))
     pl.when(me > 0)(lambda: start_halo(1))
+    loads[3].start()
+    loads[4].start()
 
     @pl.when(me == 0)
     def _():
@@ -143,10 +159,11 @@
         spread = jnp.where(diagonal, jnp.broadcast_to(row, (levels, levels)), 0.0)
         return jnp.sum(spread, axis=1, keepdims=True)
 
+    for i in (5, 6, 7, 8, 9):
+        loads[i].wait()
     sides[0] = jnp.broadcast_to(column(rates_ref[...]), (levels, 128))
     sides[1] = jnp.broadcast_to(column(thresholds_ref[...]), (levels, 128))
 
-    loads[0].wait()
     loads[1].wait()
 
     def local_terms(g, carry):
@@ -161,7 +178,7 @@
             flux = (zz + shifted(zz, 1)) * face * (1.0 / 24.0)
             source = -rate * jnp.log(1.0 + jnp.exp(hh - threshold))
             base[r, at, :] = hh - (flux - shifted(flux, nlon - 1)) + source
-            weighted = weighted + source * lat_ref[1, first + r]
+            weighted = weighted + source * row_weight(r)
         total = jnp.sum(weighted, axis=1, keepdims=True)
         part[at, :] = jnp.broadcast_to(total, (GROUP, 128))
         return carry
@@ -204,7 +221,7 @@
         scaled = jnp.concatenate([spectrum[r] * factor[r] for r in range(rows)], axis=0)
         return product(scaled, high_table, low_table)
 
-    loads[2].wait()
+    polar = jnp.logical_or(first < nlat // 4, first + rows > nlat - nlat // 4)
 
     def merid(c):
         def body(g, carry):
@@ -219,9 +236,9 @@
             previous = None
             for f in range(rows + 1):
                 face = 7.0 * (height(f - 1) + height(f)) - (height(f - 2) + height(f + 1))
-                flux = (speed(f - 1) + speed(f)) * face * lat_ref[0, first + f]
+                flux = (speed(f - 1) + speed(f)) * face * face_scale(f)
                 if f > 0:
-                    base[f - 1, at, :] -= (flux - previous) * lat_ref[2, first + f - 1]
+                    base[f - 1, at, :] -= (flux - previous) * row_scale(f - 1)
                 previous = flux
             return carry
 
@@ -244,15 +261,6 @@
         if c == 0:
             loads[3].wait()
             loads[4].wait()
-        at = pl.ds(c * width, width)
-        x = base[:, at, :].reshape(rows * width, nlon)
-        near, far = x[:, :half], x[:, half:]
-        even, odd = near + far, near - far
-        left, right = even[:, :quarter], even[:, quarter:]
-        zero = removed(left + right, quarter_t[0, 0], quarter_t[1, 0], all_factors[0])
-        two = removed(left - right, quarter_t[0, 1], quarter_t[1, 1], all_factors[1])
-        ones = removed(odd, half_t[0], half_t[1], all_factors[2])
-        even = jnp.concatenate([zero + two, zero - two], axis=1)
         if c == 0:
             def wait_sum(o, carry):
                 sum_copy(o).wait()
@@ -261,9 +269,26 @@
             lax.fori_loop(1, n, wait_sum, 0)
             total = mine[...] + jnp.sum(others[...], axis=0)
             mean = column(total[:, :levels]) * (1.0 / area)
-        kept = jnp.concatenate([near - even - ones, far - even + ones], axis=1)
-        kept = kept.reshape(rows, width, nlon) - mean[c * width : (c + 1) * width][None]
-        result[:, at, :] = kept
+        at = pl.ds(c * width, width)
+        level_mean = mean[c * width : (c + 1) * width][None]
+
+        @pl.when(polar)
+        def _():
+            x = base[:, at, :].reshape(rows * width, nlon)
+            near, far = x[:, :half], x[:, half:]
+            even, odd = near + far, near - far
+            left, right = even[:, :quarter], even[:, quarter:]
+            zero = removed(left + right, quarter_t[0, 0], quarter_t[1, 0], all_factors[0])
+            two = removed(left - right, quarter_t[0, 1], quarter_t[1, 1], all_factors[1])
+            ones = removed(odd, half_t[0], half_t[1], all_factors[2])
+            even = jnp.concatenate([zero + two, zero - two], axis=1)
+            kept = jnp.concatenate([near - even - ones, far - even + ones], axis=1)
+            result[:, at, :] = kept.reshape(rows, width, nlon) - level_mean
+
+        @pl.when(jnp.logical_not(polar))
+        def _():
+            result[:, at, :] = base[:, at, :] - level_mean
+
         store = pltpu.make_async_copy(result.at[:, at], out_hbm.at[:, at], out_sem.at[c])
         store.start()
         stores.append(store)
@@ -283,16 +308,20 @@
     rows, levels, nlon = height.shape
     table, row_sum = latitude_table(rows * n)
     quarter_t, half_t = filter_tables(nlon)
-    smem = pl.BlockSpec(memory_space=pltpu.SMEM)
-    vmem = pl.BlockSpec(memory_space=pltpu.VMEM)
-    hbm = pl.BlockSpec(memory_space=pl.ANY)
+    hbm = pl.BlockSpec(memory_space=pltpu.HBM)
+    any_space = pl.BlockSpec(memory_space=pl.ANY)
     block = pltpu.VMEM(height.shape, F32)
     return pl.pallas_call(
         functools.partial(kernel, n, nlon * row_sum),
         out_shape=jax.ShapeDtypeStruct(height.shape, F32),
-        in_specs=[smem] * 3 + [vmem] * 2 + [hbm] * 5,
-        out_specs=hbm,
+        in_specs=[hbm] * 10,
+        out_specs=any_space,
         scratch_shapes=[
+            pltpu.SMEM(table.shape, F32),
+            pltpu.SMEM(flags.shape, jnp.int32),
+            pltpu.SMEM(cutoffs.shape, jnp.int32),
+            pltpu.VMEM((1, levels), F32),
+            pltpu.VMEM((1, levels), F32),
             block, block, block,
             pltpu.VMEM(quarter_t.shape, BF),
             pltpu.VMEM(half_t.shape, BF),
@@ -305,7 +334,7 @@
             pltpu.VMEM((levels, nlon), F32),
             pltpu.VMEM((2, levels, nlon), F32),
             pltpu.VMEM((levels, nlon), F32),
-            pltpu.SemaphoreType.DMA((5,)),
+            pltpu.SemaphoreType.DMA((10,)),
             pltpu.SemaphoreType.DMA((CHUNKS,)),
             pltpu.SemaphoreType.DMA((2, CHUNKS, 2)),
             pltpu.SemaphoreType.DMA((2, CHUNKS, 2)),
@@ -313,7 +342,7 @@
             pltpu.SemaphoreType.DMA((n - 1,)),
         ],
         compiler_params=pltpu.CompilerParams(
-            collective_id=0, has_side_effects=True, vmem_limit_bytes=48 * 1024 * 1024
+            collective_id=0, has_side_effects=True, vmem_limit_bytes=67043328
         ),
     )(
         jnp.asarray(table), flags, cutoffs, rates[None, :], thresholds[None, :],

time: 32.1 us -> 26.7 us (0.83)
  local copies, waits for them, and re-layouts: 8.82 us -> 2.07 us
  Pallas kernels: 23 us -> 24.5 us
    unnamed x19 -> x1, local copies, waits for them, and re-layouts: 8.82 us -> 2.07 us
    pallas_call x1, Pallas kernels: 23 us -> 24.5 us  [local(): pl.pallas_call(functools.partial(kernel, n, nlon * row_sum), out_shape=ja...]
where the time goes in v2:
time: 26.7 us; the launch traced here: 26.6 us
  Pallas kernels  24.5 us (92%)
  local copies, waits for them, and re-layouts  2.07 us (8%)
    pallas_call x1, Pallas kernels, local(): pl.pallas_call(functools.partial(kernel, n, nlon * row_sum), out_shape=ja...  24.5 us
    unnamed x1, local copies, waits for them, and re-layouts  2.07 us

profile of v2, /device:TPU:5, one launch (start us, length us, event | category | flops | bytes accessed | tf_op | source)
XLA Modules:
  0.0 26.6 jit_solution(10250145020350774093)
XLA Ops:
  0.0 24.5 %shard_map.100 = f32[4,32,1440]{2,1,0:T(8,128)} custom-call(f32[193]{0:T(256)} %constant.6.clone.lat_hbm, s32[64]{0:T(128)} %flags_hbm.1, s32[64]{0:T(128)} %cutoffs_hbm.1, f32[1,32]{1,0:T(1,128)} %bitcast.2, f32[1,32]{1,0:T(1,128)} %bitcast.3, f32[4,32,1440]{2,1,0:T(8,128)} %h_hbm.1, f32[4,32,1440]{2,1,0:T(8,128)} %z_hbm.1, f32[4,32,1440]{2,1,0:T(8,128)} %m_hbm.1, ...), custom_call_target="tpu_custom_call" | custom-call | tf_op jit(solution)/shard_map/pallas_call | solution.py:314
  24.5 2.1 %copy.12 = f32[4,32,1440]{2,1,0:T(8,128)} copy(f32[4,32,1440]{2,1,0:T(8,128)} %shard_map.100) | data formatting | bytes 1474560

commit v3 on v2

--- a/solution.py
+++ b/solution.py
@@ -64,11 +64,11 @@
     n, area,
     lat_hbm, flags_hbm, cutoffs_hbm, rates_hbm, thresholds_hbm,
     h_hbm, z_hbm, m_hbm, quarter_hbm, half_hbm,
-    out_hbm,
+    out,
     lat_ref, flags_ref, cutoffs_ref, rates_ref, thresholds_ref,
-    h, z, m, quarter_t, half_t, base, result, sides, part, mine, others,
+    h, z, m, quarter_t, half_t, base, sides, part, mine, others,
     hl, ml, hr, mr,
-    in_sem, out_sem, halo_send, halo_recv, sum_send, sum_recv,
+    in_sem, halo_send, halo_recv, sum_send, sum_recv,
 ):
     rows, levels, nlon = h.shape
     me = lax.axis_index("lat")
@@ -245,7 +245,6 @@
         lax.fori_loop(0, width // GROUP, body, 0)
 
     mean = None
-    stores = []
     for c in range(CHUNKS):
         @pl.when(me > 0)
         def _():
@@ -283,15 +282,12 @@
             ones = removed(odd, half_t[0], half_t[1], all_factors[2])
             even = jnp.concatenate([zero + two, zero - two], axis=1)
             kept = jnp.concatenate([near - even - ones, far - even + ones], axis=1)
-            result[:, at, :] = kept.reshape(rows, width, nlon) - level_mean
+            out[:, at, :] = kept.reshape(rows, width, nlon) - level_mean
 
         @pl.when(jnp.logical_not(polar))
         def _():
-            result[:, at, :] = base[:, at, :] - level_mean
-
-        store = pltpu.make_async_copy(result.at[:, at], out_hbm.at[:, at], out_sem.at[c])
-        store.start()
-        stores.append(store)
+            out[:, at, :] = base[:, at, :] - level_mean
+
 
     def finish_halo(side):
         for c in range(CHUNKS):
@@ -300,8 +296,6 @@
 
     pl.when(me < n - 1)(lambda: finish_halo(0))
     pl.when(me > 0)(lambda: finish_halo(1))
-    for store in stores:
-        store.wait()
 
 
 def local(n, height, zonal_courant, merid_courant, rates, thresholds, flags, cutoffs):
@@ -309,13 +303,13 @@
     table, row_sum = latitude_table(rows * n)
     quarter_t, half_t = filter_tables(nlon)
     hbm = pl.BlockSpec(memory_space=pltpu.HBM)
-    any_space = pl.BlockSpec(memory_space=pl.ANY)
+    vmem = pl.BlockSpec(memory_space=pltpu.VMEM)
     block = pltpu.VMEM(height.shape, F32)
     return pl.pallas_call(
         functools.partial(kernel, n, nlon * row_sum),
-        out_shape=jax.ShapeDtypeStruct(height.shape, F32),
+        out_shape=pltpu.VMEM(height.shape, F32),
         in_specs=[hbm] * 10,
-        out_specs=any_space,
+        out_specs=vmem,
         scratch_shapes=[
             pltpu.SMEM(table.shape, F32),
             pltpu.SMEM(flags.shape, jnp.int32),
@@ -325,7 +319,7 @@
             block, block, block,
             pltpu.VMEM(quarter_t.shape, BF),
             pltpu.VMEM(half_t.shape, BF),
-            block, block,
+            block,
             pltpu.VMEM((2, levels, 128), F32),
             pltpu.VMEM((levels, 128), F32),
             pltpu.VMEM((1, 128), F32),
@@ -335,14 +329,13 @@
             pltpu.VMEM((2, levels, nlon), F32),
             pltpu.VMEM((levels, nlon), F32),
             pltpu.SemaphoreType.DMA((10,)),
-            pltpu.SemaphoreType.DMA((CHUNKS,)),
             pltpu.SemaphoreType.DMA((2, CHUNKS, 2)),
             pltpu.SemaphoreType.DMA((2, CHUNKS, 2)),
             pltpu.SemaphoreType.DMA((n - 1,)),
             pltpu.SemaphoreType.DMA((n - 1,)),
         ],
         compiler_params=pltpu.CompilerParams(
-            collective_id=0, has_side_effects=True, vmem_limit_bytes=67043328
+            collective_id=0, has_side_effects=True, vmem_limit_bytes=62 * 1024 * 1024
         ),
     )(
         jnp.asarray(table), flags, cutoffs, rates[None, :], thresholds[None, :],

time: 26.7 us -> 24.8 us (0.929)
  local copies, waits for them, and re-layouts: 2.07 us -> 0.88 us
  Pallas kernels: 24.5 us -> 23.7 us
    unnamed x1, local copies, waits for them, and re-layouts: 2.07 us -> 0.88 us
    pallas_call x1, Pallas kernels: 24.5 us -> 23.7 us  [local(): pl.pallas_call(functools.partial(kernel, n, nlon * row_sum), out_shape=pl...]
where the time goes in v3:
time: 24.8 us; the launch traced here: 24.6 us
  Pallas kernels  23.7 us (96%)
  local copies, waits for them, and re-layouts  0.88 us (4%)
    pallas_call x1, Pallas kernels, local(): pl.pallas_call(functools.partial(kernel, n, nlon * row_sum), out_shape=pl...  23.7 us
    unnamed x1, local copies, waits for them, and re-layouts  0.88 us

profile of v3, /device:TPU:5, one launch (start us, length us, event | category | flops | bytes accessed | tf_op | source)
XLA Modules:
  0.0 24.6 jit_solution(15252378791902135390)
XLA Ops:
  0.0 23.7 %shard_map.100 = f32[4,32,1440]{2,1,0:T(8,128)S(1)} custom-call(f32[193]{0:T(256)} %constant.6.clone.lat_hbm, s32[64]{0:T(128)} %flags_hbm.1, s32[64]{0:T(128)} %cutoffs_hbm.1, f32[1,32]{1,0:T(1,128)} %bitcast.2, f32[1,32]{1,0:T(1,128)} %bitcast.3, f32[4,32,1440]{2,1,0:T(8,128)} %h_hbm.1, f32[4,32,1440]{2,1,0:T(8,128)} %z_hbm.1, f32[4,32,1440]{2,1,0:T(8,128)} %m_hbm.1, ...), custom_call_target="tpu_custom_call" | custom-call | tf_op jit(solution)/shard_map/pallas_call | solution.py:308
  23.7 0.9 %copy.12 = f32[4,32,1440]{2,1,0:T(8,128)} copy(f32[4,32,1440]{2,1,0:T(8,128)S(1)} %shard_map.100) | data formatting | bytes 1474560

commit v4 on v3

--- a/solution.py
+++ b/solution.py
@@ -8,7 +8,9 @@
 from jax.experimental.pallas import tpu as pltpu
 from jax.sharding import PartitionSpec as P
 
-CHUNKS = 2
+CHUNKS = 4
+IN_FLIGHT = 3
+FILTERED = ((0, 3), (3, 4))
 GROUP = 8
 BF = jnp.bfloat16
 F32 = jnp.float32
@@ -101,12 +103,19 @@
 
     barrier = pltpu.get_barrier_semaphore()
 
-    def greet(o, c):
+    def in_group(o):
+        return me - lax.rem(me, 4) + lax.rem(me + o, 4)
+
+
+    for o in (1, 2, 3):
+        pl.semaphore_signal(barrier, inc=1, device_id={"lat": in_group(o)})
+    for o in range(4, n, 4):
         pl.semaphore_signal(barrier, inc=1, device_id={"lat": lax.rem(me + o, n)})
-        return c
-
-    lax.fori_loop(1, n, greet, 0)
-    pl.semaphore_wait(barrier, n - 1)
+    up = jnp.logical_and(lax.rem(me, 4) == 3, me < n - 1)
+    down = jnp.logical_and(lax.rem(me, 4) == 0, me > 0)
+    pl.when(up)(lambda: pl.semaphore_signal(barrier, inc=1, device_id={"lat": me + 1}))
+    pl.when(down)(lambda: pl.semaphore_signal(barrier, inc=1, device_id={"lat": me - 1}))
+    pl.semaphore_wait(barrier, 2 + n // 4 + up.astype(jnp.int32) + down.astype(jnp.int32))
 
     def halo_copies(c, side):
         at = pl.ds(c * width, width)
@@ -130,15 +139,20 @@
             for i, (src, dst) in enumerate(pairs)
         ]
 
-    def start_halo(side):
-        for c in range(CHUNKS):
-            for copy in halo_copies(c, side):
-                copy.start()
+    def each(side, chunks, act):
+        @pl.when(me < n - 1 if side == 0 else me > 0)
+        def _():
+            for c in chunks:
+                for copy in halo_copies(c, side):
+                    act(copy)
+
+    def start_halo(chunks):
+        each(0, chunks, lambda copy: copy.start())
+        each(1, chunks, lambda copy: copy.start())
 
     loads[0].wait()
     loads[2].wait()
-    pl.when(me < n - 1)(lambda: start_halo(0))
-    pl.when(me > 0)(lambda: start_halo(1))
+    start_halo(range(IN_FLIGHT))
     loads[3].start()
     loads[4].start()
 
@@ -187,19 +201,18 @@
 
     wide = lax.broadcasted_iota(jnp.int32, (levels, 128), 1)
     tall = lax.broadcasted_iota(jnp.int32, (levels, 128), 0)
-    mine[...] = jnp.sum(jnp.where(wide == tall, part[...], 0.0), axis=0, keepdims=True)
-
-    def sum_copy(o):
+    mine[0] = jnp.sum(jnp.where(wide == tall, part[...], 0.0), axis=0, keepdims=True)
+
+    def sum_copy(stage, slot, target):
         return pltpu.make_async_remote_copy(
-            mine, others.at[o - 1], sum_send.at[o - 1], sum_recv.at[o - 1],
-            device_id={"lat": lax.rem(me + o, n)},
+            mine.at[stage], others.at[slot], sum_send.at[slot], sum_recv.at[slot],
+            device_id={"lat": target},
         )
 
-    def send_sum(o, c):
-        sum_copy(o).start()
-        return c
-
-    lax.fori_loop(1, n, send_sum, 0)
+    near_sums = [sum_copy(0, o - 1, in_group(o)) for o in (1, 2, 3)]
+    far_sums = [sum_copy(1, 2 + o, lax.rem(me + 4 * o, n)) for o in range(1, n // 4)]
+    for copy in near_sums:
+        copy.start()
 
     quarter, half = nlon // 4, nlon // 2
 
@@ -217,7 +230,7 @@
     all_factors = [factors(quarter, 4, 0), factors(quarter, 4, 2), factors(half, 2, 1)]
 
     def removed(x, high_table, low_table, factor):
-        spectrum = product(x, high_table, low_table).reshape(rows, width, x.shape[1])
+        spectrum = product(x, high_table, low_table).reshape(rows, -1, x.shape[1])
         scaled = jnp.concatenate([spectrum[r] * factor[r] for r in range(rows)], axis=0)
         return product(scaled, high_table, low_table)
 
@@ -244,8 +257,7 @@
 
         lax.fori_loop(0, width // GROUP, body, 0)
 
-    mean = None
-    for c in range(CHUNKS):
+    def receive(c):
         @pl.when(me > 0)
         def _():
             for copy in halo_copies(c, 0):
@@ -256,24 +268,35 @@
             for copy in halo_copies(c, 1):
                 copy.wait_recv()
 
-        merid(c)
-        if c == 0:
+        each(0, [c], lambda copy: copy.wait_send())
+        each(1, [c], lambda copy: copy.wait_send())
+        if c + IN_FLIGHT < CHUNKS:
+            start_halo([c + IN_FLIGHT])
+
+    mean = None
+    for low, high in FILTERED:
+        for c in range(low, high):
+            receive(c)
+            merid(c)
+            if c == 0:
+                for copy in near_sums:
+                    copy.wait()
+                mine[1] = mine[0] + jnp.sum(others[:3], axis=0)
+                for copy in far_sums:
+                    copy.start()
+        if low == 0:
             loads[3].wait()
             loads[4].wait()
-        if c == 0:
-            def wait_sum(o, carry):
-                sum_copy(o).wait()
-                return carry
-
-            lax.fori_loop(1, n, wait_sum, 0)
-            total = mine[...] + jnp.sum(others[...], axis=0)
+            for copy in far_sums:
+                copy.wait()
+            total = mine[1] + jnp.sum(others[3:], axis=0)
             mean = column(total[:, :levels]) * (1.0 / area)
-        at = pl.ds(c * width, width)
-        level_mean = mean[c * width : (c + 1) * width][None]
+        at = pl.ds(low * width, (high - low) * width)
+        level_mean = mean[low * width : high * width][None]
 
         @pl.when(polar)
         def _():
-            x = base[:, at, :].reshape(rows * width, nlon)
+            x = base[:, at, :].reshape(rows * (high - low) * width, nlon)
             near, far = x[:, :half], x[:, half:]
             even, odd = near + far, near - far
             left, right = even[:, :quarter], even[:, quarter:]
@@ -282,20 +305,11 @@
             ones = removed(odd, half_t[0], half_t[1], all_factors[2])
             even = jnp.concatenate([zero + two, zero - two], axis=1)
             kept = jnp.concatenate([near - even - ones, far - even + ones], axis=1)
-            out[:, at, :] = kept.reshape(rows, width, nlon) - level_mean
+            out[:, at, :] = kept.reshape(rows, (high - low) * width, nlon) - level_mean
 
         @pl.when(jnp.logical_not(polar))
         def _():
             out[:, at, :] = base[:, at, :] - level_mean
-
-
-    def finish_halo(side):
-        for c in range(CHUNKS):
-            for copy in halo_copies(c, side):
-                copy.wait_send()
-
-    pl.when(me < n - 1)(lambda: finish_halo(0))
-    pl.when(me > 0)(lambda: finish_halo(1))
 
 
 def local(n, height, zonal_courant, merid_courant, rates, thresholds, flags, cutoffs):
@@ -322,8 +336,8 @@
             block,
             pltpu.VMEM((2, levels, 128), F32),
             pltpu.VMEM((levels, 128), F32),
-            pltpu.VMEM((1, 128), F32),
-            pltpu.VMEM((n - 1, 1, 128), F32),
+            pltpu.VMEM((2, 1, 128), F32),
+            pltpu.VMEM((2 + n // 4, 1, 128), F32),
             pltpu.VMEM((2, levels, nlon), F32),
             pltpu.VMEM((levels, nlon), F32),
             pltpu.VMEM((2, levels, nlon), F32),
@@ -331,8 +345,8 @@
             pltpu.SemaphoreType.DMA((10,)),
             pltpu.SemaphoreType.DMA((2, CHUNKS, 2)),
             pltpu.SemaphoreType.DMA((2, CHUNKS, 2)),
-            pltpu.SemaphoreType.DMA((n - 1,)),
-            pltpu.SemaphoreType.DMA((n - 1,)),
+            pltpu.SemaphoreType.DMA((2 + n // 4,)),
+            pltpu.SemaphoreType.DMA((2 + n // 4,)),
         ],
         compiler_params=pltpu.CompilerParams(
             collective_id=0, has_side_effects=True, vmem_limit_bytes=62 * 1024 * 1024

time: 24.8 us -> 27.3 us (1.10)
  the two profiles are of different devices: /device:TPU:5 before, /device:TPU:0 now
where the time goes in v4:
time: 27.3 us; the launch traced here: 27.2 us
  Pallas kernels  26.3 us (96%)
  local copies, waits for them, and re-layouts  0.88 us (3%)
    pallas_call x1, Pallas kernels, local(): pl.pallas_call(functools.partial(kernel, n, nlon * row_sum), out_shape=pl...  26.3 us
    unnamed x1, local copies, waits for them, and re-layouts  0.88 us

profile of v4, /device:TPU:0, one launch (start us, length us, event | category | flops | bytes accessed | tf_op | source)
XLA Modules:
  0.0 27.2 jit_solution(1948196964077991050)
XLA Ops:
  0.0 26.3 %shard_map.100 = f32[4,32,1440]{2,1,0:T(8,128)S(1)} custom-call(f32[193]{0:T(256)} %constant.6.clone.lat_hbm, s32[64]{0:T(128)} %flags_hbm.1, s32[64]{0:T(128)} %cutoffs_hbm.1, f32[1,32]{1,0:T(1,128)} %bitcast.2, f32[1,32]{1,0:T(1,128)} %bitcast.3, f32[4,32,1440]{2,1,0:T(8,128)} %h_hbm.1, f32[4,32,1440]{2,1,0:T(8,128)} %z_hbm.1, f32[4,32,1440]{2,1,0:T(8,128)} %m_hbm.1, ...), custom_call_target="tpu_custom_call" | custom-call | tf_op jit(solution)/shard_map/pallas_call | solution.py:322
  26.3 0.9 %copy.12 = f32[4,32,1440]{2,1,0:T(8,128)} copy(f32[4,32,1440]{2,1,0:T(8,128)S(1)} %shard_map.100) | data formatting | bytes 1474560

commit v5 on v3

--- a/solution.py
+++ b/solution.py
@@ -8,7 +8,9 @@
 from jax.experimental.pallas import tpu as pltpu
 from jax.sharding import PartitionSpec as P
 
-CHUNKS = 2
+CHUNKS = 4
+IN_FLIGHT = 3
+FILTERED = ((0, 2), (2, 4))
 GROUP = 8
 BF = jnp.bfloat16
 F32 = jnp.float32
@@ -130,15 +132,20 @@
             for i, (src, dst) in enumerate(pairs)
         ]
 
-    def start_halo(side):
-        for c in range(CHUNKS):
-            for copy in halo_copies(c, side):
-                copy.start()
+    def each(side, chunks, act):
+        @pl.when(me < n - 1 if side == 0 else me > 0)
+        def _():
+            for c in chunks:
+                for copy in halo_copies(c, side):
+                    act(copy)
+
+    def start_halo(chunks):
+        each(0, chunks, lambda copy: copy.start())
+        each(1, chunks, lambda copy: copy.start())
 
     loads[0].wait()
     loads[2].wait()
-    pl.when(me < n - 1)(lambda: start_halo(0))
-    pl.when(me > 0)(lambda: start_halo(1))
+    start_halo(range(IN_FLIGHT))
     loads[3].start()
     loads[4].start()
 
@@ -217,7 +224,7 @@
     all_factors = [factors(quarter, 4, 0), factors(quarter, 4, 2), factors(half, 2, 1)]
 
     def removed(x, high_table, low_table, factor):
-        spectrum = product(x, high_table, low_table).reshape(rows, width, x.shape[1])
+        spectrum = product(x, high_table, low_table).reshape(rows, -1, x.shape[1])
         scaled = jnp.concatenate([spectrum[r] * factor[r] for r in range(rows)], axis=0)
         return product(scaled, high_table, low_table)
 
@@ -244,8 +251,7 @@
 
         lax.fori_loop(0, width // GROUP, body, 0)
 
-    mean = None
-    for c in range(CHUNKS):
+    def receive(c):
         @pl.when(me > 0)
         def _():
             for copy in halo_copies(c, 0):
@@ -256,11 +262,19 @@
             for copy in halo_copies(c, 1):
                 copy.wait_recv()
 
-        merid(c)
-        if c == 0:
+        each(0, [c], lambda copy: copy.wait_send())
+        each(1, [c], lambda copy: copy.wait_send())
+        if c + IN_FLIGHT < CHUNKS:
+            start_halo([c + IN_FLIGHT])
+
+    mean = None
+    for low, high in FILTERED:
+        for c in range(low, high):
+            receive(c)
+            merid(c)
+        if low == 0:
             loads[3].wait()
             loads[4].wait()
-        if c == 0:
             def wait_sum(o, carry):
                 sum_copy(o).wait()
                 return carry
@@ -268,12 +282,12 @@
             lax.fori_loop(1, n, wait_sum, 0)
             total = mine[...] + jnp.sum(others[...], axis=0)
             mean = column(total[:, :levels]) * (1.0 / area)
-        at = pl.ds(c * width, width)
-        level_mean = mean[c * width : (c + 1) * width][None]
+        at = pl.ds(low * width, (high - low) * width)
+        level_mean = mean[low * width : high * width][None]
 
         @pl.when(polar)
         def _():
-            x = base[:, at, :].reshape(rows * width, nlon)
+            x = base[:, at, :].reshape(rows * (high - low) * width, nlon)
             near, far = x[:, :half], x[:, half:]
             even, odd = near + far, near - far
             left, right = even[:, :quarter], even[:, quarter:]
@@ -282,20 +296,11 @@
             ones = removed(odd, half_t[0], half_t[1], all_factors[2])
             even = jnp.concatenate([zero + two, zero - two], axis=1)
             kept = jnp.concatenate([near - even - ones, far - even + ones], axis=1)
-            out[:, at, :] = kept.reshape(rows, width, nlon) - level_mean
+            out[:, at, :] = kept.reshape(rows, (high - low) * width, nlon) - level_mean
 
         @pl.when(jnp.logical_not(polar))
         def _():
             out[:, at, :] = base[:, at, :] - level_mean
-
-
-    def finish_halo(side):
-        for c in range(CHUNKS):
-            for copy in halo_copies(c, side):
-                copy.wait_send()
-
-    pl.when(me < n - 1)(lambda: finish_halo(0))
-    pl.when(me > 0)(lambda: finish_halo(1))
 
 
 def local(n, height, zonal_courant, merid_courant, rates, thresholds, flags, cutoffs):

time: 24.8 us -> 23.3 us (0.940)
  Pallas kernels: 23.7 us -> 22.3 us
    pallas_call x1, Pallas kernels: 23.7 us -> 22.3 us  [local(): pl.pallas_call(functools.partial(kernel, n, nlon * row_sum), out_shape=pl...]
where the time goes in v5:
time: 23.3 us; the launch traced here: 23.2 us
  Pallas kernels  22.3 us (96%)
  local copies, waits for them, and re-layouts  0.88 us (4%)
    pallas_call x1, Pallas kernels, local(): pl.pallas_call(functools.partial(kernel, n, nlon * row_sum), out_shape=pl...  22.3 us
    unnamed x1, local copies, waits for them, and re-layouts  0.88 us

profile of v5, /device:TPU:5, one launch (start us, length us, event | category | flops | bytes accessed | tf_op | source)
XLA Modules:
  0.0 23.2 jit_solution(835416940390506679)
XLA Ops:
  0.0 22.3 %shard_map.100 = f32[4,32,1440]{2,1,0:T(8,128)S(1)} custom-call(f32[193]{0:T(256)} %constant.6.clone.lat_hbm, s32[64]{0:T(128)} %flags_hbm.1, s32[64]{0:T(128)} %cutoffs_hbm.1, f32[1,32]{1,0:T(1,128)} %bitcast.2, f32[1,32]{1,0:T(1,128)} %bitcast.3, f32[4,32,1440]{2,1,0:T(8,128)} %h_hbm.1, f32[4,32,1440]{2,1,0:T(8,128)} %z_hbm.1, f32[4,32,1440]{2,1,0:T(8,128)} %m_hbm.1, ...), custom_call_target="tpu_custom_call" | custom-call | tf_op jit(solution)/shard_map/pallas_call | solution.py:313
  22.3 0.9 %copy.12 = f32[4,32,1440]{2,1,0:T(8,128)} copy(f32[4,32,1440]{2,1,0:T(8,128)S(1)} %shard_map.100) | data formatting | bytes 1474560
